TPU v7x, 32 devices: a whole 2x2x4 slice. The times are simulated.
32 devices in a mesh: gx: 8 (over z, x), gz: 4 (over y, core).
Axes of the slice: x: 2, y: 2, z: 4, core: 2. Of those that a mesh axis runs over, the one named last changes fastest.
Arguments:
- velocity: float32 [3, 64, 128, 384], P(None, 'gx', 'gz'), may hold values from -6 to 6
- y_gap: float32 [385], replicated, may hold values from 0.2 to 2
Outputs:
- eddy_visc: float32 [64, 128, 384], P('gx', 'gz')
- lm_field: float32 [64, 128, 384], P('gx', 'gz')
- mm_field: float32 [64, 128, 384], P('gx', 'gz')
- coefficient: float32 [384], replicated
All inputs are finite; a program needn't handle non-finite values.
Results may differ from a plain program's by a relative error of at most 0.00002.
Values sent between devices are 32-bit elements; how exact they have to be, the bound alone decides.
A program may use at most 64 MiB of HBM per device.

v0:
```python
import jax
import jax.numpy as jnp
from jax import lax
from jax.sharding import PartitionSpec as P

WEIGHTS = (1.0, 1.0, 1.0, 2.0, 2.0, 2.0)


def extended(array, sides, width):
    for axis, dim in sides:
        size, length = (lax.axis_size(axis), array.shape[dim])
        up = [(i, (i + 1) % size) for i in range(size)]
        down = [(j, i) for i, j in up]
        last = lax.slice_in_dim(array, length - width, length, axis=dim)
        leading = lax.slice_in_dim(array, 0, width, axis=dim)
        before = lax.ppermute(last, axis, up)
        after = lax.ppermute(leading, axis, down)
        array = jnp.concatenate([before, array, after], axis=dim)
    return array


def wall_slope(values, y_gap):
    padded = jnp.pad(values, [(0, 0)] * (values.ndim - 1) + [(1, 1)])
    return (padded[..., 2:] - padded[..., :-2]) / (y_gap[:-1] + y_gap[1:])


def strain_parts(slope_x, slope_y, slope_z):
    return jnp.stack(
        [
            slope_x[0],
            slope_y[1],
            slope_z[2],
            0.5 * (slope_y[0] + slope_x[1]),
            0.5 * (slope_z[0] + slope_x[2]),
            0.5 * (slope_z[1] + slope_y[2]),
        ]
    )


def contract(first_part, second_part):
    summed = first_part[0] * second_part[0]
    for component in range(1, 6):
        summed = summed + WEIGHTS[component] * first_part[component] * second_part[component]
    return summed


def magnitude(strain):
    return jnp.sqrt(2.0 * contract(strain, strain))


def pair_products(speeds):
    return jnp.stack(
        [
            speeds[0] * speeds[0],
            speeds[1] * speeds[1],
            speeds[2] * speeds[2],
            speeds[0] * speeds[1],
            speeds[0] * speeds[2],
            speeds[1] * speeds[2],
        ]
    )


def width_square(y_gap):
    return (0.5 * (y_gap[:-1] + y_gap[1:])) ** (2.0 / 3.0)


def germano(smooth_velocity, smooth_pairs, smooth_stress, test_strain, width_sq):
    leonard = smooth_pairs - pair_products(smooth_velocity)
    model_term = 2.0 * width_sq * (smooth_stress - 4.0 * magnitude(test_strain) * test_strain)
    return (contract(leonard, model_term), contract(model_term, model_term))


def rim_strain(padded, y_gap):
    slope_x = (padded[:, 2:, 1:-1] - padded[:, :-2, 1:-1]) * 0.5
    slope_z = (padded[:, 1:-1, 2:] - padded[:, 1:-1, :-2]) * 0.5
    slope_y = wall_slope(padded[:, 1:-1, 1:-1], y_gap)
    return strain_parts(slope_x, slope_y, slope_z)


def rim_filter(values):
    along_x = 0.25 * values[:, :-2] + 0.5 * values[:, 1:-1] + 0.25 * values[:, 2:]
    return 0.25 * along_x[:, :, :-2] + 0.5 * along_x[:, :, 1:-1] + 0.25 * along_x[:, :, 2:]


def per_device(velocity, y_gap):
    width_sq = width_square(y_gap)
    padded = extended(velocity, (("gx", 1), ("gz", 2)), 2)
    strain_wide = rim_strain(padded, y_gap)
    size_wide = magnitude(strain_wide)
    inner = padded[:, 1:-1, 1:-1]
    smooth_pairs = rim_filter(pair_products(inner))
    smooth_stress = rim_filter(size_wide * strain_wide)
    smooth_wide = rim_filter(padded)
    smooth_velocity = smooth_wide[:, 1:-1, 1:-1]
    test_strain = rim_strain(smooth_wide, y_gap)
    strain_size = size_wide[1:-1, 1:-1]
    lm_field, mm_field = germano(
        smooth_velocity, smooth_pairs, smooth_stress, test_strain, width_sq
    )
    planes = velocity.shape[1] * lax.axis_size("gx") * velocity.shape[2] * lax.axis_size("gz")
    plane_pair = jnp.stack([jnp.sum(lm_field, axis=(0, 1)), jnp.sum(mm_field, axis=(0, 1))])
    total_pair = lax.psum(plane_pair, ("gx", "gz"))
    coefficient = total_pair[0] / planes / (total_pair[1] / planes + 1e-06)
    eddy_visc = coefficient * width_sq * strain_size
    return (eddy_visc, lm_field, mm_field, coefficient)


def solution(mesh):
    placed = (P(None, "gx", "gz", None), P())
    return jax.shard_map(
        per_device,
        mesh=mesh,
        in_specs=placed,
        out_specs=(P("gx", "gz", None), P("gx", "gz", None), P("gx", "gz", None), P()),
        check_vma=False,
    )
```

profile of v0, /device:TPU:0, one launch (start us, length us, event | category | flops | bytes accessed | tf_op | source)
XLA Modules:
  0.0 76.4 jit_solution(4850961541052591493)
XLA Ops:
  0.6 0.0 copy-start
  0.6 0.0 copy-start.2
  0.7 1.2 %fusion.70 = (f32[3,2,32,384]{3,2,1,0:T(8,128)S(1)}, f32[3,2,32,384]{3,2,1,0:T(8,128)S(1)}) fusion(f32[3,8,32,384]{3,2,1,0:T(8,128)} %param.2), kind=kLoop, calls=%fused_computation.159 | loop fusion | bytes 1179648 | tf_op jit(solution)/shard_map/slice | solution.py:15
  1.8 3.0 %collective-permute-start = (f32[3,2,32,384]{3,2,1,0:T(8,128)S(1)}, f32[3,2,32,384]{3,2,1,0:T(8,128)S(1)}, u32[]{:S(2)}, u32[]{:S(2)}) collective-permute-start(f32[3,2,32,384]{3,2,1,0:T(8,128)S(1)} %get-tuple-element.30), channel_id=1, source_target_pairs={{0,4},{4,8},{8,12},{12,16},{16,20},{20,24},{24,28},{28,0},{1,5},{5... | collective-permute-start | bytes 884744 | tf_op jit(solution)/shard_map/ppermute | solution.py:16
  4.9 3.1 %collective-permute-start.1 = (f32[3,2,32,384]{3,2,1,0:T(8,128)S(1)}, f32[3,2,32,384]{3,2,1,0:T(8,128)S(1)}, u32[]{:S(2)}, u32[]{:S(2)}) collective-permute-start(f32[3,2,32,384]{3,2,1,0:T(8,128)S(1)} %get-tuple-element.29), channel_id=1, source_target_pairs={{4,0},{8,4},{12,8},{16,12},{20,16},{24,20},{28,24},{0,28},{5,1},{9... | collective-permute-start | bytes 884744 | tf_op jit(solution)/shard_map/ppermute | solution.py:17
  8.0 9.5 %collective-permute-done = f32[3,2,32,384]{3,2,1,0:T(8,128)S(1)} collective-permute-done((f32[3,2,32,384]{3,2,1,0:T(8,128)S(1)}, f32[3,2,32,384]{3,2,1,0:T(8,128)S(1)}, u32[]{:S(2)}, u32[]{:S(2)}) %collective-permute-start) | collective-permute-done | bytes 294944 | tf_op jit(solution)/shard_map/ppermute | solution.py:16
  17.5 0.0 copy-done
  17.5 0.1 constant_dynamic-update-slice_fusion.1
  17.6 2.1 %collective-permute-done.1 = f32[3,2,32,384]{3,2,1,0:T(8,128)S(1)} collective-permute-done((f32[3,2,32,384]{3,2,1,0:T(8,128)S(1)}, f32[3,2,32,384]{3,2,1,0:T(8,128)S(1)}, u32[]{:S(2)}, u32[]{:S(2)}) %collective-permute-start.1) | collective-permute-done | bytes 294944 | tf_op jit(solution)/shard_map/ppermute | solution.py:17
  19.7 0.1 fusion.69
  19.8 0.1 collective-permute-start.3
  19.8 0.5 collective-permute-start.2
  20.3 0.0 copy-done.2
  20.3 0.1 fusion.58
  20.4 1.8 %collective-permute-done.3 = f32[3,12,2,384]{3,2,1,0:T(2,128)S(1)} collective-permute-done((f32[3,12,2,384]{3,2,1,0:T(2,128)S(1)}, f32[3,12,2,384]{3,2,1,0:T(2,128)S(1)}, u32[]{:S(2)}, u32[]{:S(2)}) %collective-permute-start.3) | collective-permute-done | bytes 110624 | tf_op jit(solution)/shard_map/ppermute | solution.py:17
  22.3 3.0 %collective-permute-done.2 = f32[3,12,2,384]{3,2,1,0:T(2,128)S(1)} collective-permute-done((f32[3,12,2,384]{3,2,1,0:T(2,128)S(1)}, f32[3,12,2,384]{3,2,1,0:T(2,128)S(1)}, u32[]{:S(2)}, u32[]{:S(2)}) %collective-permute-start.2) | collective-permute-done | bytes 110624 | tf_op jit(solution)/shard_map/ppermute | solution.py:16
  25.2 0.3 pad_maximum_fusion
  25.5 0.3 fusion.15
  25.8 0.3 fusion.18
  26.0 0.5 fusion.16
  26.6 0.4 fusion.22
  27.0 0.1 multiply_dynamic-update-slice_fusion.8
  27.1 1.3 %fusion.12 = (f32[3,10,34,384]{3,2,1,0:T(8,128)S(1)}, f32[3,10,34,384]{3,2,1,0:T(8,128)S(1)}) fusion(f32[3,10,34,384]{3,2,1,0:T(8,128)S(1)} %get-tuple-element.22, f32[384]{0:T(512)S(1)} %get-tuple-element.9, f32[3,12,32,384]{3,2,1,0:T(8,128)S(1)} %constant_dynamic-update-slice_fusion, f32[3,12,2,384]{3,2,1,0:T(2,128)S(1)} %collective-permute-done.2, ...), kind=kLoop, calls=%fused_computation.27 | loop fusion | flops 2350080 | bytes 6692352 | tf_op jit(solution)/shard_map/div | solution.py:24
  28.5 0.6 fusion.29
  29.2 0.1 multiply_dynamic-update-slice_fusion.1
  29.3 0.1 multiply_dynamic-update-slice_fusion
  29.4 0.3 broadcast_multiply_fusion
  29.6 0.4 fusion
  30.1 0.7 fusion.21
  30.8 0.4 fusion.36
  31.5 0.1 multiply_dynamic-update-slice_fusion.14
  31.5 0.1 multiply_dynamic-update-slice_fusion.13
  31.6 0.1 multiply_dynamic-update-slice_fusion.12
  31.7 0.1 multiply_dynamic-update-slice_fusion.7
  31.8 0.1 multiply_dynamic-update-slice_fusion.6
  31.8 0.1 multiply_dynamic-update-slice_fusion.5
  31.9 0.1 multiply_dynamic-update-slice_fusion.4
  32.0 0.1 multiply_dynamic-update-slice_fusion.3
  32.2 0.4 fusion.2
  32.6 0.9 %fusion.9 = f32[6,8,32,384]{3,2,1,0:T(8,128)S(1)} fusion(f32[6,8,32,384]{3,2,1,0:T(8,128)S(1)} %multiply_dynamic-update-slice_fusion.12, f32[6,8,34,384]{3,2,1,0:T(8,128)S(1)} %fusion.2), kind=kLoop, calls=%fused_computation.21 | loop fusion | flops 3538944 | bytes 11796480 | tf_op jit(solution)/shard_map/sub | solution.py:69
  33.5 0.9 %fusion.6 = f32[6,8,32,384]{3,2,1,0:T(8,128)S(1)} fusion(f32[6,8,34,384]{3,2,1,0:T(8,128)S(1)} %fusion, f32[6,8,32,384]{3,2,1,0:T(8,128)S(1)} %multiply_dynamic-update-slice_fusion.9, f32[8,32,384]{2,1,0:T(8,128)S(1)} %get-tuple-element.19, f32[384]{0:T(512)S(1)} %get-tuple-element.8), kind=kLoop, calls=%fused_computation.15 | loop fusion | flops 4718592 | bytes 12191232 | tf_op jit(solution)/shard_map/mul | solution.py:70
  34.4 1.4 %fusion.65 = (f32[384]{0:T(512)S(1)}, f32[8,32,384]{2,1,0:T(8,128)}, f32[384]{0:T(512)S(1)}, f32[8,32,384]{2,1,0:T(8,128)}) fusion(f32[6,8,32,384]{3,2,1,0:T(8,128)S(1)} %fusion.6, f32[6,8,32,384]{3,2,1,0:T(8,128)S(1)} %fusion.9), kind=kLoop, calls=%fused_computation.156 | loop fusion | flops 2948352 | bytes 5508096 | tf_op jit(solution)/shard_map/reduce_sum | solution.py:102
  35.8 39.4 %psum.7 = f32[2,384]{1,0:T(2,128)S(1)} all-reduce(f32[2,384]{1,0:T(2,128)S(1)} %pad_maximum_fusion.3), channel_id=1, replica_groups=mesh['gx'=8,'gz'=4] {'gx','gz'}, use_global_device_ids=true, to_apply=%region_2.3 | all-reduce | flops 768 | bytes 6144 | tf_op jit(solution)/shard_map/psum | solution.py:103
  75.2 0.0 copy-start.1
  75.2 1.1 %fusion.44 = f32[8,32,384]{2,1,0:T(8,128)} fusion(f32[10,34,384]{2,1,0:T(8,128)S(1)} %get-tuple-element.14, f32[10,34,384]{2,1,0:T(8,128)S(1)} %get-tuple-element.12, f32[10,34,384]{2,1,0:T(8,128)S(1)} %get-tuple-element.16, f32[10,34,384]{2,1,0:T(8,128)S(1)} %broadcast_multiply_fusion.1, f32[10,34,384]{2,1,0:T(8,128)S(1)} %bitcast.69, f32[384]{0:T(512)S(1)} %fusion.57), kind=kLoop, calls=%fused_computation.103 | loop fusion | flops 983040 | bytes 2360832 | tf_op jit(solution)/shard_map/mul | solution.py:105
  76.4 0.0 copy-done.1
  (19 shorter events, 0.6 us)
Async XLA Ops:
  0.6 16.8 %copy-start = (f32[3,8,32,384]{3,2,1,0:T(8,128)S(1)}, f32[3,8,32,384]{3,2,1,0:T(8,128)}, u32[]{:S(2)}) copy-start(f32[3,8,32,384]{3,2,1,0:T(8,128)} %param.2) | copy-start | bytes 3538948
  0.6 19.7 %copy-start.2 = (f32[385]{0:T(512)S(1)}, f32[385]{0:T(512)}, u32[]{:S(2)}) copy-start(f32[385]{0:T(512)} %param.3) | copy-start | bytes 4624
  1.8 15.6 %collective-permute-start = (f32[3,2,32,384]{3,2,1,0:T(8,128)S(1)}, f32[3,2,32,384]{3,2,1,0:T(8,128)S(1)}, u32[]{:S(2)}, u32[]{:S(2)}) collective-permute-start(f32[3,2,32,384]{3,2,1,0:T(8,128)S(1)} %get-tuple-element.30), channel_id=1, source_target_pairs={{0,4},{4,8},{8,12},{12,16},{16,20},{20,24},{24,28},{28,0},{1,5},{5... | collective-permute-start | bytes 884744 | tf_op jit(solution)/shard_map/ppermute | solution.py:16
  4.9 14.8 %collective-permute-start.1 = (f32[3,2,32,384]{3,2,1,0:T(8,128)S(1)}, f32[3,2,32,384]{3,2,1,0:T(8,128)S(1)}, u32[]{:S(2)}, u32[]{:S(2)}) collective-permute-start(f32[3,2,32,384]{3,2,1,0:T(8,128)S(1)} %get-tuple-element.29), channel_id=1, source_target_pairs={{4,0},{8,4},{12,8},{16,12},{20,16},{24,20},{28,24},{0,28},{5,1},{9... | collective-permute-start | bytes 884744 | tf_op jit(solution)/shard_map/ppermute | solution.py:17
  19.8 2.5 %collective-permute-start.3 = (f32[3,12,2,384]{3,2,1,0:T(2,128)S(1)}, f32[3,12,2,384]{3,2,1,0:T(2,128)S(1)}, u32[]{:S(2)}, u32[]{:S(2)}) collective-permute-start(f32[3,12,2,384]{3,2,1,0:T(2,128)S(1)} %get-tuple-element.28), channel_id=1, source_target_pairs={{1,0},{2,1},{3,2},{0,3},{5,4},{6,5},{7,6},{4,7},{9,8},{10,9},{11,1... | collective-permute-start | bytes 331784 | tf_op jit(solution)/shard_map/ppermute | solution.py:17
  19.8 5.4 %collective-permute-start.2 = (f32[3,12,2,384]{3,2,1,0:T(2,128)S(1)}, f32[3,12,2,384]{3,2,1,0:T(2,128)S(1)}, u32[]{:S(2)}, u32[]{:S(2)}) collective-permute-start(f32[3,12,2,384]{3,2,1,0:T(2,128)S(1)} %get-tuple-element.27), channel_id=1, source_target_pairs={{0,1},{1,2},{2,3},{3,0},{4,5},{5,6},{6,7},{7,4},{8,9},{9,10},{10,1... | collective-permute-start | bytes 331784 | tf_op jit(solution)/shard_map/ppermute | solution.py:16
  75.2 1.2 %copy-start.1 = (f32[384]{0:T(512)}, f32[384]{0:T(512)S(1)}, u32[]{:S(2)}) copy-start(f32[384]{0:T(512)S(1)} %fusion.61) | copy-start | bytes 4612
where the time goes:
time: 76.6 us; the launch traced here: 76.4 us
  blocking collectives  39.4 us (51%)
  waiting for transfers between devices  16.4 us (21%)
  other arithmetic  11.4 us (15%)
  starting transfers between devices  6.68 us (9%)
  local copies, waits for them, and re-layouts  1.59 us (2%)
  between operations  0.97 us (1%)
    psum x1, blocking collectives, per_device(): total_pair = lax.psum(plane_pair, ('gx', 'gz'))  39.4 us
    ppermute x2, waiting for transfers between devices, extended(): before = lax.ppermute(last, axis, up)  12.4 us
    ppermute x2, waiting for transfers between devices, extended(): after = lax.ppermute(leading, axis, down)  3.91 us
    ppermute x2, starting transfers between devices, extended(): before = lax.ppermute(last, axis, up)  3.52 us
    ppermute x2, starting transfers between devices, extended(): after = lax.ppermute(leading, axis, down)  3.16 us
    div x2, other arithmetic, wall_slope(): return (padded[..., 2:] - padded[..., :-2]) / (y_gap[:-1] + y_gap[1:])  1.94 us
  transfers between devices with their start and end apart: 4, of which 4 were waited for; matrix products, arithmetic and copies ran while one was open for 0% of the time, Pallas kernels for 0%

commit v1 on v0

v1 whole, which is shorter than its diff:
```python
import functools

import jax
import jax.numpy as jnp
from jax import lax
from jax.experimental import pallas as pl
from jax.experimental.pallas import tpu as pltpu
from jax.sharding import PartitionSpec as P

MESH = pl.DeviceIdType.MESH
LANES = 128
RIM = 8


def kernel(gxn, gzn, cells, coef_ref, vel_ref, eddy_ref, lm_ref, mm_ref, out_coef_ref,
           pad, zvel, zpair, zstress, slope, tslope, size_s, lm_s, mm_s, eddy_s, sums, acc_z, acc_x,
           local_sem, xs_sem, xr_sem, ks_sem, kr_sem, cs_sem, cr_sem,
           zs_sem, zr_sem, ws_sem, wr_sem, out_sem):
    gx, gz = lax.axis_index("gx"), lax.axis_index("gz")
    nx, nz, ny = vel_ref.shape[1:]
    wide = nz + RIM
    right, left = lax.rem(gx + 1, gxn), lax.rem(gx + gxn - 1, gxn)
    after, before = lax.rem(gz + 1, gzn), lax.rem(gz + gzn - 1, gzn)

    load = pltpu.make_async_copy(vel_ref, pad.at[:, 2:nx + 2, 0:nz], local_sem)
    load.start()
    barrier = pltpu.get_barrier_semaphore()
    for d in range(1, gxn):
        pl.semaphore_signal(barrier, inc=1, device_id=(lax.rem(gx + d, gxn), gz), device_id_type=MESH)
    for d in range(1, gzn):
        pl.semaphore_signal(barrier, inc=1, device_id=(gx, lax.rem(gz + d, gzn)), device_id_type=MESH)
    sums[...] = jnp.zeros_like(sums)
    load.wait()
    pl.semaphore_wait(barrier, gxn + gzn - 2)

    def remote(src, dst, send, recv, device):
        return pltpu.make_async_remote_copy(
            src_ref=src, dst_ref=dst, send_sem=send, recv_sem=recv,
            device_id=device, device_id_type=MESH)

    pieces = ((0, 8), (nz - 8, 8), (8, nz - 16))
    x_copies = []
    for n, (start, count) in enumerate(pieces):
        ks = pl.ds(start, count)
        x_copies.append((
            remote(pad.at[:, nx:nx + 2, ks], pad.at[:, 0:2, ks], xs_sem.at[n, 0], xr_sem.at[n, 0], (right, gz)),
            remote(pad.at[:, 2:4, ks], pad.at[:, nx + 2:nx + 4, ks], xs_sem.at[n, 1], xr_sem.at[n, 1], (left, gz))))
    k_up = remote(pad.at[:, 2:nx + 2, nz - 2:nz], pad.at[:, 2:nx + 2, wide - 2:wide], ks_sem.at[0], kr_sem.at[0], (gx, after))
    k_down = remote(pad.at[:, 2:nx + 2, 0:2], pad.at[:, 2:nx + 2, nz:nz + 2], ks_sem.at[1], kr_sem.at[1], (gx, before))
    k_up.start()
    k_down.start()
    for pair in x_copies:
        for copy in pair:
            copy.start()

    half_ahead, half_back = coef_ref[0:1, :], coef_ref[1:2, :]

    def filtered(f):
        twice = f + pltpu.roll(f, 1, 0)
        return twice + pltpu.roll(twice, wide - 1, 0)

    def lane_slope(f):
        return pltpu.roll(f, ny - 1, 1) * half_ahead - pltpu.roll(f, 1, 1) * half_back

    def tiles():
        return [pl.ds(t, LANES) for t in range(0, ny, LANES)]

    def smooth_row(r):
        for c in range(3):
            for cols in tiles():
                zvel[c, r, :, cols] = filtered(pad[c, r, :, cols])

    def first(r):
        for c in range(3):
            slope[c] = lane_slope(pad[c, r])
        for cols in tiles():
            u = [pad[c, r, :, cols] for c in range(3)]
            a = [pad[c, r + 1, :, cols] - pad[c, r - 1, :, cols] for c in range(3)]
            b = []
            for c in range(3):
                prev, nxt = pltpu.roll(u[c], 1, 0), pltpu.roll(u[c], wide - 1, 0)
                b.append(nxt - prev)
                zvel[c, r, :, cols] = (nxt + prev) + 2.0 * u[c]
            d = [slope[c, :, cols] for c in range(3)]
            strain = [a[0], d[1], b[2], d[0] + a[1], b[0] + a[2], b[1] + d[2]]
            square = [s * s for s in strain]
            size = jnp.sqrt(0.5 * (square[0] + square[1] + square[2]) + 0.25 * (square[3] + square[4] + square[5]))
            size_s[r, :, cols] = size[:nz]
            for n in range(6):
                zstress[n, r, :, cols] = filtered(size * strain[n])[:nz]
            for n, (i, j) in enumerate(((0, 0), (1, 1), (2, 2), (0, 1), (0, 2), (1, 2))):
                zpair[n, r, :, cols] = filtered(u[i] * u[j])[:nz]

    def second(r):
        for c in range(3):
            v = (zvel[c, r - 1] + zvel[c, r + 1]) + 2.0 * zvel[c, r]
            tslope[c] = v
            slope[c] = lane_slope(v)
        for cols in tiles():
            w = coef_ref[2:3, cols]
            w2 = coef_ref[3:4, cols]
            v_wide = [tslope[c, :, cols] for c in range(3)]
            v = [f[:nz] for f in v_wide]
            a = [(zvel[c, r + 2, 0:nz, cols] - zvel[c, r - 2, 0:nz, cols])
                 + 2.0 * (zvel[c, r + 1, 0:nz, cols] - zvel[c, r - 1, 0:nz, cols]) for c in range(3)]
            b = [(pltpu.roll(f, wide - 1, 0) - pltpu.roll(f, 1, 0))[:nz] for f in v_wide]
            d = [slope[c, 0:nz, cols] for c in range(3)]
            test = [a[0], d[1], b[2], d[0] + a[1], b[0] + a[2], b[1] + d[2]]
            square = [s * s for s in test]
            q = 0.25 * jnp.sqrt(0.5 * (square[0] + square[1] + square[2]) + 0.25 * (square[3] + square[4] + square[5]))
            lm, mm_diag, mm_off = 0.0, 0.0, 0.0
            for n, (i, j) in enumerate(((0, 0), (1, 1), (2, 2), (0, 1), (0, 2), (1, 2))):
                stress = (zstress[n, r - 1, :, cols] + zstress[n, r + 1, :, cols]) + 2.0 * zstress[n, r, :, cols]
                model = stress - q * test[n]
                pair = (zpair[n, r - 1, :, cols] + zpair[n, r + 1, :, cols]) + 2.0 * zpair[n, r, :, cols]
                lm = lm + (pair - v[i] * v[j] * 0.0625) * model
                if n < 3:
                    mm_diag = mm_diag + model * model
                else:
                    mm_off = mm_off + model * model
            lm = lm * w
            mm = (mm_diag + 0.5 * mm_off) * w2
            lm_s[r - 2, :, cols] = lm
            mm_s[r - 2, :, cols] = mm
            for n, f in enumerate((lm, mm)):
                sums[n, :, cols] += jnp.sum(f.reshape(nz // 8, 8, LANES), axis=0)

    def over(lo, hi, body):
        def step(r, carry):
            body(r)
            return carry
        lax.fori_loop(lo, hi, step, 0)

    k_up.wait_recv()
    k_down.wait_recv()
    over(3, nx + 1, first)
    for n in (0, 1):
        for copy in x_copies[n]:
            copy.wait_recv()
    corners = []
    for n, rows in enumerate((slice(0, 2), slice(nx + 2, nx + 4))):
        corners.append(remote(pad.at[:, rows, nz - 2:nz], pad.at[:, rows, wide - 2:wide], cs_sem.at[n, 0], cr_sem.at[n, 0], (gx, after)))
        corners.append(remote(pad.at[:, rows, 0:2], pad.at[:, rows, nz:nz + 2], cs_sem.at[n, 1], cr_sem.at[n, 1], (gx, before)))
    for copy in corners:
        copy.start()
    smooth_row(2)
    smooth_row(nx + 1)
    over(4, nx, second)
    for copy in x_copies[2]:
        copy.wait_recv()
    for copy in corners:
        copy.wait_recv()

    def edge(n, carry):
        first(lax.select(n < 2, n + 1, n + nx - 1))
        return carry

    def edge_second(n, carry):
        second(lax.select(n < 2, n + 2, n + nx - 2))
        return carry

    lax.fori_loop(0, 4, edge, 0)
    smooth_row(0)
    smooth_row(nx + 3)
    lax.fori_loop(0, 4, edge_second, 0)

    def exchange(acc, me, size, send, recv, device):
        copies = []
        for d in range(1, size):
            there = lax.rem(me + d, size)
            copy = remote(acc.at[me], acc.at[me], send.at[d - 1], recv.at[d - 1], device(there))
            copy.start()
            copies.append(copy)
        return copies

    def collect(acc, me, size, send, recv, device):
        for d in range(1, size):
            source = lax.rem(me + size - d, size)
            remote(acc.at[source], acc.at[source], send.at[d - 1], recv.at[d - 1], device(source)).wait_recv()
        total = acc[0]
        for n in range(1, size):
            total = total + acc[n]
        return total

    z_args = (acc_z, gz, gzn, zs_sem, zr_sem, lambda other: (gx, other))
    x_args = (acc_x, gx, gxn, ws_sem, wr_sem, lambda other: (other, gz))
    acc_z[gz] = jnp.sum(sums[...], axis=1)
    z_copies = exchange(*z_args)
    lm_out = pltpu.make_async_copy(lm_s, lm_ref, out_sem.at[0])
    mm_out = pltpu.make_async_copy(mm_s, mm_ref, out_sem.at[1])
    lm_out.start()
    mm_out.start()
    acc_x[gx] = collect(*z_args)
    w_copies = exchange(*x_args)
    total = collect(*x_args)
    coefficient = total[0:1] / cells / (total[1:2] / cells + 1e-06)
    out_coef_ref[...] = coefficient
    factor = coefficient * coef_ref[4:5, :]
    eddy_outs = []
    for r in range(nx):
        eddy_s[r] = factor * size_s[r + 2]
        copy = pltpu.make_async_copy(eddy_s.at[r], eddy_ref.at[r], out_sem.at[2 + r])
        copy.start()
        eddy_outs.append(copy)
    k_up.wait_send()
    k_down.wait_send()
    for pair in x_copies:
        for copy in pair:
            copy.wait_send()
    for copy in corners + z_copies + w_copies:
        copy.wait_send()
    lm_out.wait()
    mm_out.wait()
    for copy in eddy_outs:
        copy.wait()


def per_device(velocity, y_gap):
    gxn, gzn = lax.axis_size("gx"), lax.axis_size("gz")
    _, nx, nz, ny = velocity.shape
    cells = float(nx * gxn * nz * gzn)
    span = y_gap[:-1] + y_gap[1:]
    width_sq = (0.5 * span) ** (2.0 / 3.0)
    at = lax.iota(jnp.int32, ny)
    coefs = jnp.stack([
        jnp.where(at == ny - 1, 0.0, 2.0 / span),
        jnp.where(at == 0, 0.0, 2.0 / span),
        width_sq / 256.0,
        width_sq * width_sq / 256.0,
        width_sq, width_sq, width_sq, width_sq,
    ])
    field = jax.ShapeDtypeStruct((nx, nz, ny), jnp.float32)
    f32 = jnp.float32
    wide = nz + RIM
    dma = pltpu.SemaphoreType.DMA
    eddy, lm, mm, coefficient = pl.pallas_call(
        functools.partial(kernel, gxn, gzn, cells),
        out_shape=(field, field, field, jax.ShapeDtypeStruct((1, ny), f32)),
        in_specs=[pl.BlockSpec(memory_space=pltpu.VMEM), pl.BlockSpec(memory_space=pl.ANY)],
        out_specs=(pl.BlockSpec(memory_space=pl.ANY),) * 3 + (pl.BlockSpec(memory_space=pltpu.VMEM),),
        scratch_shapes=[
            pltpu.VMEM((3, nx + 4, wide, ny), f32),
            pltpu.VMEM((3, nx + 4, wide, ny), f32),
            pltpu.VMEM((6, nx + 4, nz, ny), f32),
            pltpu.VMEM((6, nx + 4, nz, ny), f32),
            pltpu.VMEM((3, wide, ny), f32),
            pltpu.VMEM((3, wide, ny), f32),
            pltpu.VMEM((nx + 4, nz, ny), f32),
            pltpu.VMEM((nx, nz, ny), f32),
            pltpu.VMEM((nx, nz, ny), f32),
            pltpu.VMEM((nx, nz, ny), f32),
            pltpu.VMEM((2, 8, ny), f32),
            pltpu.VMEM((gzn, 2, ny), f32),
            pltpu.VMEM((gxn, 2, ny), f32),
            dma, dma((3, 2)), dma((3, 2)), dma((2,)), dma((2,)), dma((2, 2)), dma((2, 2)),
            dma((max(gzn - 1, 1),)), dma((max(gzn - 1, 1),)), dma((max(gxn - 1, 1),)), dma((max(gxn - 1, 1),)),
            dma((2 + nx,)),
        ],
        compiler_params=pltpu.CompilerParams(collective_id=0, has_side_effects=True),
    )(coefs, velocity)
    return (eddy, lm, mm, coefficient.reshape(ny))


def solution(mesh):
    placed = (P(None, "gx", "gz", None), P())
    return jax.shard_map(
        per_device,
        mesh=mesh,
        in_specs=placed,
        out_specs=(P("gx", "gz", None), P("gx", "gz", None), P("gx", "gz", None), P()),
        check_vma=False,
    )
```

time: 76.6 us -> 39.4 us (0.51)
  blocking collectives: 39.4 us -> 0 us
  Pallas kernels: 0 us -> 31.3 us
  waiting for transfers between devices: 16.4 us -> 0 us
  other arithmetic: 11.4 us -> 2.13 us
  starting transfers between devices: 6.68 us -> 0 us
  local copies, waits for them, and re-layouts: 1.59 us -> 4.93 us
    psum x1 -> x0, blocking collectives: 39.4 us -> none  [per_device(): total_pair = lax.psum(plane_pair, ('gx', 'gz'))]
    pallas_call x0 -> x1, Pallas kernels: none -> 31.3 us  [per_device(): pl.pallas_call(functools.partial(kernel, gxn, gzn, cells), out_shape=(fie...]
    ppermute x4 -> x0, waiting for transfers between devices: 16.4 us -> none  [the longest x2 12.4 us: extended(): before = lax.ppermute(last, axis, up)]
    ppermute x4 -> x0, starting transfers between devices: 6.68 us -> none  [the longest x2 3.52 us: extended(): before = lax.ppermute(last, axis, up)]
    mul x10 -> x0, other arithmetic: 4.09 us -> none  [the longest x2 1.13 us: per_device(): eddy_visc = coefficient * width_sq * strain_size]
    unnamed x13 -> x5, local copies, waits for them, and re-layouts: 0.29 us -> 4.28 us
    add x4 -> x0, other arithmetic: 1.61 us -> none  [the longest x3 1.07 us: rim_filter(): 0.25 * values[:, :-2] + 0.5 * values[:, 1:-1] + 0.25 * values[:, 2:]]
    reduce_sum x1 -> x0, other arithmetic: 1.42 us -> none  [per_device(): jnp.sum(lm_field, axis=(0, 1))]
  transfers between devices with their start and end apart: 4 -> 0, of which waited for: 4 -> 0; matrix products, arithmetic and copies ran while one was open for 0% -> 0% of each run, Pallas kernels for 0% -> 0%
where the time goes in v1:
time: 39.4 us; the launch traced here: 39 us
  Pallas kernels  31.3 us (79%)
  local copies, waits for them, and re-layouts  4.93 us (13%)
  other arithmetic  2.13 us (5%)
  between operations  0.7 us (2%)
    pallas_call x1, Pallas kernels, per_device(): pl.pallas_call(functools.partial(kernel, gxn, gzn, cells), out_shape=(fie...  31.3 us
    unnamed x5, local copies, waits for them, and re-layouts  4.28 us
    pallas_call x1, other arithmetic, per_device(): pl.pallas_call(functools.partial(kernel, gxn, gzn, cells), out_shape=(fie...  1.28 us
    div x1, other arithmetic, per_device(): width_sq * width_sq / 256.0  0.85 us

profile of v1, /device:TPU:0, one launch (start us, length us, event | category | flops | bytes accessed | tf_op | source)
XLA Modules:
  0.0 39.0 jit_solution(71969931007446962)
XLA Ops:
  0.6 0.9 %multiply_multiply_fusion = (f32[384]{0:T(512)S(1)}, f32[384]{0:T(512)S(1)}, f32[384]{0:T(512)S(1)}, f32[384]{0:T(512)S(1)}) fusion(f32[385]{0:T(512)} %param.3), kind=kLoop, calls=%fused_computation | loop fusion | flops 2688 | bytes 9216 | tf_op jit(solution)/shard_map/div | solution.py:229
  1.5 0.6 %stack.26.coef_ref = f32[8,384]{1,0:T(8,128)} concatenate(f32[1,384]{1,0:T(1,128)S(1)} %stack.21, f32[1,384]{1,0:T(1,128)S(1)} %stack.22, f32[1,384]{1,0:T(1,128)S(1)} %stack.23, f32[1,384]{1,0:T(1,128)S(1)} %stack.24, f32[1,384]{1,0:T(1,128)S(1)} %stack.25, f32[1,384]{1,0:T(1,128)S(1)} %stack.25, f32[1,384]{1,0:T(1,128)S(1)} %stack.25, f32[1,384]{1,0:T(1,128)S(1)} %stack.25), dimensions={0} | concatenate | bytes 24576 | tf_op jit(solution)/shard_map/stack | solution.py:225
  2.2 31.3 %shard_map.57 = (f32[8,32,384]{2,1,0:T(8,128)}, f32[8,32,384]{2,1,0:T(8,128)}, f32[8,32,384]{2,1,0:T(8,128)}, f32[1,384]{1,0:T(1,128)}) custom-call(f32[8,384]{1,0:T(8,128)} %stack.26.coef_ref, f32[3,8,32,384]{3,2,1,0:T(8,128)} %vel_ref.1), custom_call_target="tpu_custom_call" | custom-call | tf_op jit(solution)/shard_map/pallas_call | solution.py:236
  33.5 0.0 copy-start
  33.5 1.3 %reduce = f32[384]{0:T(512)} reduce(f32[1,384]{1,0:T(1,128)} %get-tuple-element.11, f32[]{:T(128)} %constant.16), dimensions={0}, to_apply=%get-tuple-element.11.reduce_sub_computation | reduce | bytes 3076 | tf_op jit(solution)/shard_map/pallas_call | solution.py:236
  34.8 1.8 %copy.9 = f32[8,32,384]{2,1,0:T(8,128)} copy(f32[8,32,384]{2,1,0:T(8,128)} %get-tuple-element.24) | data formatting | bytes 786432
  36.5 1.8 %copy.10 = f32[8,32,384]{2,1,0:T(8,128)} copy(f32[8,32,384]{2,1,0:T(8,128)} %get-tuple-element.25) | data formatting | bytes 786432
  38.3 0.0 copy-done
  38.3 0.7 %copy.11 = f32[8,32,384]{2,1,0:T(8,128)} copy(f32[8,32,384]{2,1,0:T(8,128)S(1)} %copy-done) | data formatting | bytes 786432
  (6 shorter events, 0.0 us)
Async XLA Ops:
  33.5 4.8 %copy-start = (f32[8,32,384]{2,1,0:T(8,128)S(1)}, f32[8,32,384]{2,1,0:T(8,128)}, u32[]{:S(2)}) copy-start(f32[8,32,384]{2,1,0:T(8,128)} %get-tuple-element.26) | copy-start | bytes 1179652

commit v2 on v1

--- a/solution.py
+++ b/solution.py
@@ -12,10 +12,31 @@
 RIM = 8
 
 
-def kernel(gxn, gzn, cells, coef_ref, vel_ref, eddy_ref, lm_ref, mm_ref, out_coef_ref,
-           pad, zvel, zpair, zstress, slope, tslope, size_s, lm_s, mm_s, eddy_s, sums, acc_z, acc_x,
+def width_square(span):
+    return jnp.exp(jnp.log(0.5 * span) * (2.0 / 3.0))
+
+
+def finish(size_ref, lm_ref, mm_ref, coef_ref, gap_ref, eddy_out, lm_out, mm_out, coef_out, eddy_s, sem):
+    nx, _, ny = size_ref.shape
+    copies = [pltpu.make_async_copy(lm_ref, lm_out, sem.at[0]), pltpu.make_async_copy(mm_ref, mm_out, sem.at[1])]
+    for copy in copies:
+        copy.start()
+    factor = coef_ref[...] * width_square(gap_ref[:, 0:ny] + gap_ref[:, 1:ny + 1])
+    for r in range(0, nx, 2):
+        rows = pl.ds(r, 2)
+        eddy_s[rows] = factor * size_ref[rows]
+        copy = pltpu.make_async_copy(eddy_s.at[rows], eddy_out.at[rows], sem.at[2 + r // 2])
+        copy.start()
+        copies.append(copy)
+    coef_out[...] = coef_ref[...].reshape(ny)
+    for copy in copies:
+        copy.wait()
+
+
+def kernel(gxn, gzn, cells, gap_ref, vel_ref, size_s, lm_s, mm_s, out_coef_ref,
+           pad, zvel, zpair, zstress, slope, tslope, coef_ref, sums, acc_z, acc_x,
            local_sem, xs_sem, xr_sem, ks_sem, kr_sem, cs_sem, cr_sem,
-           zs_sem, zr_sem, ws_sem, wr_sem, out_sem):
+           zs_sem, zr_sem, ws_sem, wr_sem):
     gx, gz = lax.axis_index("gx"), lax.axis_index("gz")
     nx, nz, ny = vel_ref.shape[1:]
     wide = nz + RIM
@@ -30,6 +51,14 @@
     for d in range(1, gzn):
         pl.semaphore_signal(barrier, inc=1, device_id=(gx, lax.rem(gz + d, gzn)), device_id_type=MESH)
     sums[...] = jnp.zeros_like(sums)
+    span = gap_ref[:, 0:ny] + gap_ref[:, 1:ny + 1]
+    at = lax.broadcasted_iota(jnp.int32, (1, ny), 1)
+    width_sq = width_square(span)
+    inverse = 2.0 / span
+    coef_ref[0:1] = jnp.where(at == ny - 1, 0.0, inverse)
+    coef_ref[1:2] = jnp.where(at == 0, 0.0, inverse)
+    coef_ref[2:3] = width_sq * (1.0 / 256.0)
+    coef_ref[3:4] = width_sq * width_sq * (1.0 / 256.0)
     load.wait()
     pl.semaphore_wait(barrier, gxn + gzn - 2)
 
@@ -38,13 +67,14 @@
             src_ref=src, dst_ref=dst, send_sem=send, recv_sem=recv,
             device_id=device, device_id_type=MESH)
 
-    pieces = ((0, 8), (nz - 8, 8), (8, nz - 16))
+    pieces = ((1, 0, nz), (0, 0, 8), (0, nz - 8, 8), (0, 8, nz - 16))
     x_copies = []
-    for n, (start, count) in enumerate(pieces):
+    for n, (near, start, count) in enumerate(pieces):
         ks = pl.ds(start, count)
+        low, high = near, 1 - near
         x_copies.append((
-            remote(pad.at[:, nx:nx + 2, ks], pad.at[:, 0:2, ks], xs_sem.at[n, 0], xr_sem.at[n, 0], (right, gz)),
-            remote(pad.at[:, 2:4, ks], pad.at[:, nx + 2:nx + 4, ks], xs_sem.at[n, 1], xr_sem.at[n, 1], (left, gz))))
+            remote(pad.at[:, nx + low, ks], pad.at[:, low, ks], xs_sem.at[n, 0], xr_sem.at[n, 0], (right, gz)),
+            remote(pad.at[:, 2 + high, ks], pad.at[:, nx + 2 + high, ks], xs_sem.at[n, 1], xr_sem.at[n, 1], (left, gz))))
     k_up = remote(pad.at[:, 2:nx + 2, nz - 2:nz], pad.at[:, 2:nx + 2, wide - 2:wide], ks_sem.at[0], kr_sem.at[0], (gx, after))
     k_down = remote(pad.at[:, 2:nx + 2, 0:2], pad.at[:, 2:nx + 2, nz:nz + 2], ks_sem.at[1], kr_sem.at[1], (gx, before))
     k_up.start()
@@ -70,7 +100,7 @@
             for cols in tiles():
                 zvel[c, r, :, cols] = filtered(pad[c, r, :, cols])
 
-    def first(r):
+    def first(r, inside=True):
         for c in range(3):
             slope[c] = lane_slope(pad[c, r])
         for cols in tiles():
@@ -85,7 +115,8 @@
             strain = [a[0], d[1], b[2], d[0] + a[1], b[0] + a[2], b[1] + d[2]]
             square = [s * s for s in strain]
             size = jnp.sqrt(0.5 * (square[0] + square[1] + square[2]) + 0.25 * (square[3] + square[4] + square[5]))
-            size_s[r, :, cols] = size[:nz]
+            if inside:
+                size_s[r - 2, :, cols] = size[:nz]
             for n in range(6):
                 zstress[n, r, :, cols] = filtered(size * strain[n])[:nz]
             for n, (i, j) in enumerate(((0, 0), (1, 1), (2, 2), (0, 1), (0, 2), (1, 2))):
@@ -134,35 +165,45 @@
     k_up.wait_recv()
     k_down.wait_recv()
     over(3, nx + 1, first)
-    for n in (0, 1):
-        for copy in x_copies[n]:
-            copy.wait_recv()
-    corners = []
-    for n, rows in enumerate((slice(0, 2), slice(nx + 2, nx + 4))):
-        corners.append(remote(pad.at[:, rows, nz - 2:nz], pad.at[:, rows, wide - 2:wide], cs_sem.at[n, 0], cr_sem.at[n, 0], (gx, after)))
-        corners.append(remote(pad.at[:, rows, 0:2], pad.at[:, rows, nz:nz + 2], cs_sem.at[n, 1], cr_sem.at[n, 1], (gx, before)))
-    for copy in corners:
-        copy.start()
     smooth_row(2)
     smooth_row(nx + 1)
     over(4, nx, second)
-    for copy in x_copies[2]:
-        copy.wait_recv()
+
+    def pass_on(layer, low, high):
+        copies = []
+        for n, row in enumerate((low, high)):
+            copies.append(remote(pad.at[:, row, nz - 2:nz], pad.at[:, row, wide - 2:wide], cs_sem.at[layer, n, 0], cr_sem.at[layer, n, 0], (gx, after)))
+            copies.append(remote(pad.at[:, row, 0:2], pad.at[:, row, nz:nz + 2], cs_sem.at[layer, n, 1], cr_sem.at[layer, n, 1], (gx, before)))
+        for copy in copies:
+            copy.start()
+        return copies
+
+    def both(low, high, body):
+        def step(n, carry):
+            body(lax.select(n == 0, low, high))
+            return carry
+        lax.fori_loop(0, 2, step, 0)
+
+    for copy in x_copies[0]:
+        copy.wait_recv()
+    corners = pass_on(0, 1, nx + 2)
     for copy in corners:
         copy.wait_recv()
-
-    def edge(n, carry):
-        first(lax.select(n < 2, n + 1, n + nx - 1))
-        return carry
-
-    def edge_second(n, carry):
-        second(lax.select(n < 2, n + 2, n + nx - 2))
-        return carry
-
-    lax.fori_loop(0, 4, edge, 0)
-    smooth_row(0)
-    smooth_row(nx + 3)
-    lax.fori_loop(0, 4, edge_second, 0)
+    both(2, nx + 1, first)
+    for n in (1, 2):
+        for copy in x_copies[n]:
+            copy.wait_recv()
+    far = pass_on(1, 0, nx + 3)
+    both(1, nx + 2, smooth_row)
+    both(3, nx, second)
+    for copy in far:
+        copy.wait_recv()
+    for copy in x_copies[3]:
+        copy.wait_recv()
+    corners = corners + far
+    both(1, nx + 2, functools.partial(first, inside=False))
+    both(0, nx + 3, smooth_row)
+    both(2, nx + 1, second)
 
     def exchange(acc, me, size, send, recv, device):
         copies = []
@@ -186,22 +227,11 @@
     x_args = (acc_x, gx, gxn, ws_sem, wr_sem, lambda other: (other, gz))
     acc_z[gz] = jnp.sum(sums[...], axis=1)
     z_copies = exchange(*z_args)
-    lm_out = pltpu.make_async_copy(lm_s, lm_ref, out_sem.at[0])
-    mm_out = pltpu.make_async_copy(mm_s, mm_ref, out_sem.at[1])
-    lm_out.start()
-    mm_out.start()
     acc_x[gx] = collect(*z_args)
     w_copies = exchange(*x_args)
     total = collect(*x_args)
     coefficient = total[0:1] / cells / (total[1:2] / cells + 1e-06)
     out_coef_ref[...] = coefficient
-    factor = coefficient * coef_ref[4:5, :]
-    eddy_outs = []
-    for r in range(nx):
-        eddy_s[r] = factor * size_s[r + 2]
-        copy = pltpu.make_async_copy(eddy_s.at[r], eddy_ref.at[r], out_sem.at[2 + r])
-        copy.start()
-        eddy_outs.append(copy)
     k_up.wait_send()
     k_down.wait_send()
     for pair in x_copies:
@@ -209,35 +239,25 @@
             copy.wait_send()
     for copy in corners + z_copies + w_copies:
         copy.wait_send()
-    lm_out.wait()
-    mm_out.wait()
-    for copy in eddy_outs:
-        copy.wait()
 
 
 def per_device(velocity, y_gap):
     gxn, gzn = lax.axis_size("gx"), lax.axis_size("gz")
     _, nx, nz, ny = velocity.shape
     cells = float(nx * gxn * nz * gzn)
-    span = y_gap[:-1] + y_gap[1:]
-    width_sq = (0.5 * span) ** (2.0 / 3.0)
-    at = lax.iota(jnp.int32, ny)
-    coefs = jnp.stack([
-        jnp.where(at == ny - 1, 0.0, 2.0 / span),
-        jnp.where(at == 0, 0.0, 2.0 / span),
-        width_sq / 256.0,
-        width_sq * width_sq / 256.0,
-        width_sq, width_sq, width_sq, width_sq,
-    ])
     field = jax.ShapeDtypeStruct((nx, nz, ny), jnp.float32)
     f32 = jnp.float32
     wide = nz + RIM
     dma = pltpu.SemaphoreType.DMA
-    eddy, lm, mm, coefficient = pl.pallas_call(
+    gaps = y_gap.reshape(1, ny + 1)
+    near = pl.BlockSpec(memory_space=pltpu.VMEM)
+    far = pl.BlockSpec(memory_space=pl.ANY)
+    held = pltpu.VMEM((nx, nz, ny), f32)
+    size, lm, mm, coefficient = pl.pallas_call(
         functools.partial(kernel, gxn, gzn, cells),
-        out_shape=(field, field, field, jax.ShapeDtypeStruct((1, ny), f32)),
-        in_specs=[pl.BlockSpec(memory_space=pltpu.VMEM), pl.BlockSpec(memory_space=pl.ANY)],
-        out_specs=(pl.BlockSpec(memory_space=pl.ANY),) * 3 + (pl.BlockSpec(memory_space=pltpu.VMEM),),
+        out_shape=(held, held, held, pltpu.VMEM((1, ny), f32)),
+        in_specs=[near, far],
+        out_specs=(near,) * 4,
         scratch_shapes=[
             pltpu.VMEM((3, nx + 4, wide, ny), f32),
             pltpu.VMEM((3, nx + 4, wide, ny), f32),
@@ -245,20 +265,24 @@
             pltpu.VMEM((6, nx + 4, nz, ny), f32),
             pltpu.VMEM((3, wide, ny), f32),
             pltpu.VMEM((3, wide, ny), f32),
-            pltpu.VMEM((nx + 4, nz, ny), f32),
-            pltpu.VMEM((nx, nz, ny), f32),
-            pltpu.VMEM((nx, nz, ny), f32),
-            pltpu.VMEM((nx, nz, ny), f32),
+            pltpu.VMEM((8, ny), f32),
             pltpu.VMEM((2, 8, ny), f32),
             pltpu.VMEM((gzn, 2, ny), f32),
             pltpu.VMEM((gxn, 2, ny), f32),
-            dma, dma((3, 2)), dma((3, 2)), dma((2,)), dma((2,)), dma((2, 2)), dma((2, 2)),
+            dma, dma((4, 2)), dma((4, 2)), dma((2,)), dma((2,)), dma((2, 2, 2)), dma((2, 2, 2)),
             dma((max(gzn - 1, 1),)), dma((max(gzn - 1, 1),)), dma((max(gxn - 1, 1),)), dma((max(gxn - 1, 1),)),
-            dma((2 + nx,)),
         ],
-        compiler_params=pltpu.CompilerParams(collective_id=0, has_side_effects=True),
-    )(coefs, velocity)
-    return (eddy, lm, mm, coefficient.reshape(ny))
+        compiler_params=pltpu.CompilerParams(
+            collective_id=0, has_side_effects=True, vmem_limit_bytes=40 * 2**20),
+    )(gaps, pltpu.with_memory_space_constraint(velocity, pltpu.HBM))
+    return pl.pallas_call(
+        finish,
+        out_shape=(field, field, field, jax.ShapeDtypeStruct((ny,), f32)),
+        in_specs=[near] * 5,
+        out_specs=(far, far, far, near),
+        scratch_shapes=[pltpu.VMEM((nx, nz, ny), f32), dma((2 + (nx + 1) // 2,))],
+        compiler_params=pltpu.CompilerParams(vmem_limit_bytes=8 * 2**20),
+    )(size, lm, mm, coefficient, gaps)
 
 
 def solution(mesh):

time: 39.4 us -> 34.3 us (0.87)
  local copies, waits for them, and re-layouts: 4.93 us -> 0.67 us
  other arithmetic: 2.13 us -> 0 us
  Pallas kernels: 31.3 us -> 32.8 us
    unnamed x5 -> x2, local copies, waits for them, and re-layouts: 4.28 us -> 0.67 us
    pallas_call x1 -> x2, Pallas kernels: 31.3 us -> 32.8 us  [the longest x1 31.1 us: per_device(): pl.pallas_call(functools.partial(kernel, gxn, gzn, cells), out_shape=(hel...]
    pallas_call x1 -> x0, other arithmetic: 1.28 us -> none  [per_device(): pl.pallas_call(functools.partial(kernel, gxn, gzn, cells), out_shape=(fie...]
    div x1 -> x0, other arithmetic: 0.85 us -> none  [per_device(): width_sq * width_sq / 256.0]
    another operation x6 -> x0, local copies, waits for them, and re-layouts: 0.64 us -> none  [per_device(): jnp.stack([jnp.where(at == ny - 1, 0.0, 2.0 / span), jnp.where(at == 0, 0...]
where the time goes in v2:
time: 34.3 us; the launch traced here: 34.1 us
  Pallas kernels  32.8 us (96%)
  local copies, waits for them, and re-layouts  0.67 us (2%)
  between operations  0.65 us (2%)
    pallas_call x1, Pallas kernels, per_device(): pl.pallas_call(functools.partial(kernel, gxn, gzn, cells), out_shape=(hel...  31.1 us
    pallas_call x1, Pallas kernels, per_device(): pl.pallas_call(finish, out_shape=(field, field, field, jax.ShapeDtypeStru...  1.61 us

profile of v2, /device:TPU:0, one launch (start us, length us, event | category | flops | bytes accessed | tf_op | source)
XLA Modules:
  0.0 34.1 jit_solution(18153155985009304617)
XLA Ops:
  0.6 0.0 copy-start
  0.6 0.7 %copy-done = f32[385]{0:T(512)S(1)} copy-done((f32[385]{0:T(512)S(1)}, f32[385]{0:T(512)}, u32[]{:S(2)}) %copy-start) | copy-done | bytes 1564
  1.3 31.1 %shard_map.57 = (f32[8,32,384]{2,1,0:T(8,128)S(1)}, f32[8,32,384]{2,1,0:T(8,128)S(1)}, f32[8,32,384]{2,1,0:T(8,128)S(1)}, f32[1,384]{1,0:T(1,128)S(1)}) custom-call(f32[1,385]{1,0:T(1,128)S(1)} %bitcast.1, f32[3,8,32,384]{3,2,1,0:T(8,128)} %vel_ref.1), custom_call_target="tpu_custom_call" | custom-call | tf_op jit(solution)/shard_map/pallas_call | solution.py:256
  32.5 1.6 %shard_map.58 = (f32[8,32,384]{2,1,0:T(8,128)}, f32[8,32,384]{2,1,0:T(8,128)}, f32[8,32,384]{2,1,0:T(8,128)}, f32[384]{0:T(512)}) custom-call(f32[8,32,384]{2,1,0:T(8,128)S(1)} %get-tuple-element.8.size_ref, f32[8,32,384]{2,1,0:T(8,128)S(1)} %get-tuple-element.9.lm_ref, f32[8,32,384]{2,1,0:T(8,128)S(1)} %get-tuple-element.10.mm_ref, ...), custom_call_target="tpu_custom_call" | custom-call | tf_op jit(solution)/shard_map/pallas_call | solution.py:278
Async XLA Ops:
  0.6 0.7 %copy-start = (f32[385]{0:T(512)S(1)}, f32[385]{0:T(512)}, u32[]{:S(2)}) copy-start(f32[385]{0:T(512)} %param.3) | copy-start | bytes 4624

commit v3 on v2

--- a/solution.py
+++ b/solution.py
@@ -16,26 +16,26 @@
     return jnp.exp(jnp.log(0.5 * span) * (2.0 / 3.0))
 
 
-def finish(size_ref, lm_ref, mm_ref, coef_ref, gap_ref, eddy_out, lm_out, mm_out, coef_out, eddy_s, sem):
+def finish(size_ref, lm_ref, mm_ref, coef_ref, eddy_out, lm_out, mm_out, coef_out, eddy_s, sem):
     nx, _, ny = size_ref.shape
     copies = [pltpu.make_async_copy(lm_ref, lm_out, sem.at[0]), pltpu.make_async_copy(mm_ref, mm_out, sem.at[1])]
     for copy in copies:
         copy.start()
-    factor = coef_ref[...] * width_square(gap_ref[:, 0:ny] + gap_ref[:, 1:ny + 1])
+    factor = coef_ref[1:2]
     for r in range(0, nx, 2):
         rows = pl.ds(r, 2)
         eddy_s[rows] = factor * size_ref[rows]
         copy = pltpu.make_async_copy(eddy_s.at[rows], eddy_out.at[rows], sem.at[2 + r // 2])
         copy.start()
         copies.append(copy)
-    coef_out[...] = coef_ref[...].reshape(ny)
+    coef_out[...] = coef_ref[0:1].reshape(ny)
     for copy in copies:
         copy.wait()
 
 
-def kernel(gxn, gzn, cells, gap_ref, vel_ref, size_s, lm_s, mm_s, out_coef_ref,
+def kernel(gxn, gzn, cells, gap_hbm, vel_ref, size_s, lm_s, mm_s, out_coef_ref,
            pad, zvel, zpair, zstress, slope, tslope, coef_ref, sums, acc_z, acc_x,
-           local_sem, xs_sem, xr_sem, ks_sem, kr_sem, cs_sem, cr_sem,
+           gap_ref, gap_sem, local_sem, xs_sem, xr_sem, ks_sem, kr_sem, cs_sem, cr_sem,
            zs_sem, zr_sem, ws_sem, wr_sem):
     gx, gz = lax.axis_index("gx"), lax.axis_index("gz")
     nx, nz, ny = vel_ref.shape[1:]
@@ -45,12 +45,15 @@
 
     load = pltpu.make_async_copy(vel_ref, pad.at[:, 2:nx + 2, 0:nz], local_sem)
     load.start()
+    gap_load = pltpu.make_async_copy(gap_hbm, gap_ref, gap_sem)
+    gap_load.start()
     barrier = pltpu.get_barrier_semaphore()
     for d in range(1, gxn):
         pl.semaphore_signal(barrier, inc=1, device_id=(lax.rem(gx + d, gxn), gz), device_id_type=MESH)
     for d in range(1, gzn):
         pl.semaphore_signal(barrier, inc=1, device_id=(gx, lax.rem(gz + d, gzn)), device_id_type=MESH)
     sums[...] = jnp.zeros_like(sums)
+    gap_load.wait()
     span = gap_ref[:, 0:ny] + gap_ref[:, 1:ny + 1]
     at = lax.broadcasted_iota(jnp.int32, (1, ny), 1)
     width_sq = width_square(span)
@@ -59,6 +62,7 @@
     coef_ref[1:2] = jnp.where(at == 0, 0.0, inverse)
     coef_ref[2:3] = width_sq * (1.0 / 256.0)
     coef_ref[3:4] = width_sq * width_sq * (1.0 / 256.0)
+    coef_ref[4:5] = width_sq
     load.wait()
     pl.semaphore_wait(barrier, gxn + gzn - 2)
 
@@ -67,14 +71,15 @@
             src_ref=src, dst_ref=dst, send_sem=send, recv_sem=recv,
             device_id=device, device_id_type=MESH)
 
-    pieces = ((1, 0, nz), (0, 0, 8), (0, nz - 8, 8), (0, 8, nz - 16))
+    pieces = ((slice(0, 2), 0, 8), (slice(0, 2), nz - 8, 8), (slice(1, 2), 8, nz - 16), (slice(0, 1), 8, nz - 16))
     x_copies = []
-    for n, (near, start, count) in enumerate(pieces):
+    for n, (layers, start, count) in enumerate(pieces):
         ks = pl.ds(start, count)
-        low, high = near, 1 - near
+        low, high = layers.start, 2 - layers.stop
+        deep = layers.stop - layers.start
         x_copies.append((
-            remote(pad.at[:, nx + low, ks], pad.at[:, low, ks], xs_sem.at[n, 0], xr_sem.at[n, 0], (right, gz)),
-            remote(pad.at[:, 2 + high, ks], pad.at[:, nx + 2 + high, ks], xs_sem.at[n, 1], xr_sem.at[n, 1], (left, gz))))
+            remote(pad.at[:, nx + low:nx + low + deep, ks], pad.at[:, low:low + deep, ks], xs_sem.at[n, 0], xr_sem.at[n, 0], (right, gz)),
+            remote(pad.at[:, 2 + high:2 + high + deep, ks], pad.at[:, nx + 2 + high:nx + 2 + high + deep, ks], xs_sem.at[n, 1], xr_sem.at[n, 1], (left, gz))))
     k_up = remote(pad.at[:, 2:nx + 2, nz - 2:nz], pad.at[:, 2:nx + 2, wide - 2:wide], ks_sem.at[0], kr_sem.at[0], (gx, after))
     k_down = remote(pad.at[:, 2:nx + 2, 0:2], pad.at[:, 2:nx + 2, nz:nz + 2], ks_sem.at[1], kr_sem.at[1], (gx, before))
     k_up.start()
@@ -169,38 +174,30 @@
     smooth_row(nx + 1)
     over(4, nx, second)
 
-    def pass_on(layer, low, high):
-        copies = []
-        for n, row in enumerate((low, high)):
-            copies.append(remote(pad.at[:, row, nz - 2:nz], pad.at[:, row, wide - 2:wide], cs_sem.at[layer, n, 0], cr_sem.at[layer, n, 0], (gx, after)))
-            copies.append(remote(pad.at[:, row, 0:2], pad.at[:, row, nz:nz + 2], cs_sem.at[layer, n, 1], cr_sem.at[layer, n, 1], (gx, before)))
-        for copy in copies:
-            copy.start()
-        return copies
-
     def both(low, high, body):
         def step(n, carry):
             body(lax.select(n == 0, low, high))
             return carry
         lax.fori_loop(0, 2, step, 0)
 
-    for copy in x_copies[0]:
+    for n in (0, 1):
+        for copy in x_copies[n]:
+            copy.wait_recv()
+    corners = []
+    for n, rows in enumerate((slice(0, 2), slice(nx + 2, nx + 4))):
+        corners.append(remote(pad.at[:, rows, nz - 2:nz], pad.at[:, rows, wide - 2:wide], cs_sem.at[n, 0], cr_sem.at[n, 0], (gx, after)))
+        corners.append(remote(pad.at[:, rows, 0:2], pad.at[:, rows, nz:nz + 2], cs_sem.at[n, 1], cr_sem.at[n, 1], (gx, before)))
+    for copy in corners:
+        copy.start()
+    for copy in x_copies[2]:
         copy.wait_recv()
-    corners = pass_on(0, 1, nx + 2)
     for copy in corners:
         copy.wait_recv()
     both(2, nx + 1, first)
-    for n in (1, 2):
-        for copy in x_copies[n]:
-            copy.wait_recv()
-    far = pass_on(1, 0, nx + 3)
     both(1, nx + 2, smooth_row)
     both(3, nx, second)
-    for copy in far:
-        copy.wait_recv()
     for copy in x_copies[3]:
         copy.wait_recv()
-    corners = corners + far
     both(1, nx + 2, functools.partial(first, inside=False))
     both(0, nx + 3, smooth_row)
     both(2, nx + 1, second)
@@ -231,7 +228,8 @@
     w_copies = exchange(*x_args)
     total = collect(*x_args)
     coefficient = total[0:1] / cells / (total[1:2] / cells + 1e-06)
-    out_coef_ref[...] = coefficient
+    out_coef_ref[0:1] = coefficient
+    out_coef_ref[1:2] = coefficient * coef_ref[4:5]
     k_up.wait_send()
     k_down.wait_send()
     for pair in x_copies:
@@ -255,8 +253,8 @@
     held = pltpu.VMEM((nx, nz, ny), f32)
     size, lm, mm, coefficient = pl.pallas_call(
         functools.partial(kernel, gxn, gzn, cells),
-        out_shape=(held, held, held, pltpu.VMEM((1, ny), f32)),
-        in_specs=[near, far],
+        out_shape=(held, held, held, pltpu.VMEM((2, ny), f32)),
+        in_specs=[far, far],
         out_specs=(near,) * 4,
         scratch_shapes=[
             pltpu.VMEM((3, nx + 4, wide, ny), f32),
@@ -269,20 +267,21 @@
             pltpu.VMEM((2, 8, ny), f32),
             pltpu.VMEM((gzn, 2, ny), f32),
             pltpu.VMEM((gxn, 2, ny), f32),
-            dma, dma((4, 2)), dma((4, 2)), dma((2,)), dma((2,)), dma((2, 2, 2)), dma((2, 2, 2)),
+            pltpu.VMEM((1, ny + 1), f32), dma,
+            dma, dma((4, 2)), dma((4, 2)), dma((2,)), dma((2,)), dma((2, 2)), dma((2, 2)),
             dma((max(gzn - 1, 1),)), dma((max(gzn - 1, 1),)), dma((max(gxn - 1, 1),)), dma((max(gxn - 1, 1),)),
         ],
         compiler_params=pltpu.CompilerParams(
             collective_id=0, has_side_effects=True, vmem_limit_bytes=40 * 2**20),
-    )(gaps, pltpu.with_memory_space_constraint(velocity, pltpu.HBM))
+    )(pltpu.with_memory_space_constraint(gaps, pltpu.HBM), pltpu.with_memory_space_constraint(velocity, pltpu.HBM))
     return pl.pallas_call(
         finish,
         out_shape=(field, field, field, jax.ShapeDtypeStruct((ny,), f32)),
-        in_specs=[near] * 5,
+        in_specs=[near] * 4,
         out_specs=(far, far, far, near),
         scratch_shapes=[pltpu.VMEM((nx, nz, ny), f32), dma((2 + (nx + 1) // 2,))],
         compiler_params=pltpu.CompilerParams(vmem_limit_bytes=8 * 2**20),
-    )(size, lm, mm, coefficient, gaps)
+    )(size, lm, mm, coefficient)
 
 
 def solution(mesh):

time: 34.3 us -> 31.4 us (0.915)
  Pallas kernels: 32.8 us -> 30.6 us
  local copies, waits for them, and re-layouts: 0.67 us -> 0 us
    pallas_call x1, Pallas kernels: 31.1 us -> 29 us  [per_device(): pl.pallas_call(functools.partial(kernel, gxn, gzn, cells), out_shape=(hel...]
    unnamed x2 -> x0, local copies, waits for them, and re-layouts: 0.67 us -> none
where the time goes in v3:
time: 31.4 us; the launch traced here: 31.2 us
  Pallas kernels  30.6 us (97%)
  between operations  0.64 us (2%)
    pallas_call x1, Pallas kernels, per_device(): pl.pallas_call(functools.partial(kernel, gxn, gzn, cells), out_shape=(hel...  29 us
    pallas_call x1, Pallas kernels, per_device(): pl.pallas_call(finish, out_shape=(field, field, field, jax.ShapeDtypeStru...  1.61 us

profile of v3, /device:TPU:0, one launch (start us, length us, event | category | flops | bytes accessed | tf_op | source)
XLA Modules:
  0.0 31.2 jit_solution(7617022002490845795)
XLA Ops:
  0.6 29.0 %shard_map.57 = (f32[8,32,384]{2,1,0:T(8,128)S(1)}, f32[8,32,384]{2,1,0:T(8,128)S(1)}, f32[8,32,384]{2,1,0:T(8,128)S(1)}, f32[2,384]{1,0:T(2,128)S(1)}) custom-call(f32[1,385]{1,0:T(1,128)} %bitcast.1, f32[3,8,32,384]{3,2,1,0:T(8,128)} %vel_ref.1), custom_call_target="tpu_custom_call" | custom-call | tf_op jit(solution)/shard_map/pallas_call | solution.py:254
  29.6 1.6 %shard_map.58 = (f32[8,32,384]{2,1,0:T(8,128)}, f32[8,32,384]{2,1,0:T(8,128)}, f32[8,32,384]{2,1,0:T(8,128)}, f32[384]{0:T(512)}) custom-call(f32[8,32,384]{2,1,0:T(8,128)S(1)} %get-tuple-element.8.size_ref, f32[8,32,384]{2,1,0:T(8,128)S(1)} %get-tuple-element.9.lm_ref, f32[8,32,384]{2,1,0:T(8,128)S(1)} %get-tuple-element.10.mm_ref, ...), custom_call_target="tpu_custom_call" | custom-call | tf_op jit(solution)/shard_map/pallas_call | solution.py:277

commit v4 on v3

--- a/solution.py
+++ b/solution.py
@@ -18,14 +18,17 @@
 
 def finish(size_ref, lm_ref, mm_ref, coef_ref, eddy_out, lm_out, mm_out, coef_out, eddy_s, sem):
     nx, _, ny = size_ref.shape
-    copies = [pltpu.make_async_copy(lm_ref, lm_out, sem.at[0]), pltpu.make_async_copy(mm_ref, mm_out, sem.at[1])]
+    copies = []
+    for r in range(nx):
+        copies.append(pltpu.make_async_copy(lm_ref.at[r], lm_out.at[r], sem.at[nx + r]))
+        copies.append(pltpu.make_async_copy(mm_ref.at[r], mm_out.at[r], sem.at[2 * nx + r]))
     for copy in copies:
         copy.start()
     factor = coef_ref[1:2]
     for r in range(0, nx, 2):
         rows = pl.ds(r, 2)
         eddy_s[rows] = factor * size_ref[rows]
-        copy = pltpu.make_async_copy(eddy_s.at[rows], eddy_out.at[rows], sem.at[2 + r // 2])
+        copy = pltpu.make_async_copy(eddy_s.at[rows], eddy_out.at[rows], sem.at[r // 2])
         copy.start()
         copies.append(copy)
     coef_out[...] = coef_ref[0:1].reshape(ny)
@@ -48,7 +51,7 @@
     gap_load = pltpu.make_async_copy(gap_hbm, gap_ref, gap_sem)
     gap_load.start()
     barrier = pltpu.get_barrier_semaphore()
-    for d in range(1, gxn):
+    for d in sorted(range(1, gxn), key=lambda d: abs(2 * d - gxn)):
         pl.semaphore_signal(barrier, inc=1, device_id=(lax.rem(gx + d, gxn), gz), device_id_type=MESH)
     for d in range(1, gzn):
         pl.semaphore_signal(barrier, inc=1, device_id=(gx, lax.rem(gz + d, gzn)), device_id_type=MESH)
@@ -204,7 +207,7 @@
 
     def exchange(acc, me, size, send, recv, device):
         copies = []
-        for d in range(1, size):
+        for d in sorted(range(1, size), key=lambda d: abs(2 * d - size)):
             there = lax.rem(me + d, size)
             copy = remote(acc.at[me], acc.at[me], send.at[d - 1], recv.at[d - 1], device(there))
             copy.start()
@@ -279,7 +282,7 @@
         out_shape=(field, field, field, jax.ShapeDtypeStruct((ny,), f32)),
         in_specs=[near] * 4,
         out_specs=(far, far, far, near),
-        scratch_shapes=[pltpu.VMEM((nx, nz, ny), f32), dma((2 + (nx + 1) // 2,))],
+        scratch_shapes=[pltpu.VMEM((nx, nz, ny), f32), dma((3 * nx,))],
         compiler_params=pltpu.CompilerParams(vmem_limit_bytes=8 * 2**20),
     )(size, lm, mm, coefficient)
 

time: 31.4 us -> 31.7 us (level)
  no operation moved by 1% of the time
where the time goes in v4:
time: 31.7 us; the launch traced here: 31.6 us
  Pallas kernels  30.9 us (97%)
  between operations  0.64 us (2%)
    pallas_call x1, Pallas kernels, per_device(): pl.pallas_call(functools.partial(kernel, gxn, gzn, cells), out_shape=(hel...  29.1 us
    pallas_call x1, Pallas kernels, per_device(): pl.pallas_call(finish, out_shape=(field, field, field, jax.ShapeDtypeStru...  1.77 us

profile of v4, /device:TPU:0, one launch (start us, length us, event | category | flops | bytes accessed | tf_op | source)
XLA Modules:
  0.0 31.6 jit_solution(16416261923862908711)
XLA Ops:
  0.6 29.1 %shard_map.57 = (f32[8,32,384]{2,1,0:T(8,128)S(1)}, f32[8,32,384]{2,1,0:T(8,128)S(1)}, f32[8,32,384]{2,1,0:T(8,128)S(1)}, f32[2,384]{1,0:T(2,128)S(1)}) custom-call(f32[1,385]{1,0:T(1,128)} %bitcast.1, f32[3,8,32,384]{3,2,1,0:T(8,128)} %vel_ref.1), custom_call_target="tpu_custom_call" | custom-call | tf_op jit(solution)/shard_map/pallas_call | solution.py:257
  29.8 1.8 %shard_map.58 = (f32[8,32,384]{2,1,0:T(8,128)}, f32[8,32,384]{2,1,0:T(8,128)}, f32[8,32,384]{2,1,0:T(8,128)}, f32[384]{0:T(512)}) custom-call(f32[8,32,384]{2,1,0:T(8,128)S(1)} %get-tuple-element.8.size_ref, f32[8,32,384]{2,1,0:T(8,128)S(1)} %get-tuple-element.9.lm_ref, f32[8,32,384]{2,1,0:T(8,128)S(1)} %get-tuple-element.10.mm_ref, ...), custom_call_target="tpu_custom_call" | custom-call | tf_op jit(solution)/shard_map/pallas_call | solution.py:280
